TPU v7x, 128 devices: a whole 4x4x4 slice. The times are simulated.
128 devices in a mesh: img: 32 (over y, z, core), grp: 4 (over x).
Axes of the slice: x: 4, y: 4, z: 4, core: 2. Of those that a mesh axis runs over, the one named last changes fastest.
Arguments:
- images: bfloat16 [49152, 9216], P(('img', 'grp')), may hold values from -64 to 64, as said below
- expansion_basis: bfloat16 [9216, 960], P(None, 'img'), may hold values from -0.0625 to 0.0625
- block_sizes: int32 [16], replicated, may hold values from 1 to 80, 480 in all
- keep_count: int32 [16], replicated, may hold values from 1 to 8
- start_block: float32 [16, 80, 8], replicated, may hold values from -6 to 6
Outputs:
- features: float32 [49152, 256], P(('img', 'grp'))
- values: float32 [16, 8], replicated
Inputs may be any that keep to these rules, and one draw needn't show every extreme that they name: `images`: pixel values of order one. `block_sizes`: the 16 sizes sum to 480.
All inputs are finite; a program needn't handle non-finite values.
Results may differ from a plain program's by a relative error of at most 0.025.
Values may be sent and summed in bfloat16 or wider, within the bound.
A program may use at most 128 MiB of HBM per device.

v0:
```python
import jax
import jax.numpy as jnp
from jax import lax
from jax.sharding import Mesh
from jax.sharding import PartitionSpec as P

NMAX = 80
L = 16
S = 480
KMAX = 8
ITERS = 3
IMG = ("img_0", "img_1", "img_2")
IMG_GRP = ("img_0", "img_1", "img_2", "grp")
HIGH = lax.Precision.HIGHEST


def cut_along(shard, dim, peers):
    shape = shard.shape
    tiles = shard.reshape(*shape[:dim], peers, shape[dim] // peers, *shape[dim + 1 :])
    return jnp.moveaxis(tiles, dim, 0)


def sum_at_owner(shard, axis, dim):
    peers = lax.axis_size(axis)
    tiles = lax.all_to_all(cut_along(shard, dim, peers), axis, 0, 0, tiled=True)
    return jnp.sum(tiles, axis=0)


def summed_rows(shard, axes, dim):
    far, near = axes
    tiles = cut_along(shard, dim, lax.axis_size(far))
    nearer = sum_at_owner(tiles, near, dim + 1)
    arrived = lax.all_to_all(nearer, far, split_axis=0, concat_axis=0, tiled=True)
    return arrived.sum(axis=0)


def padded_to(lines, peers):
    spare = -len(lines) % peers
    return jnp.pad(lines, [(0, spare)] + [(0, 0)] * (lines.ndim - 1))


def sent_to_all(shard, axis):
    peers = lax.axis_size(axis)
    return lax.all_to_all(
        jnp.broadcast_to(shard[None], (peers, *shard.shape)), axis, 0, 0, tiled=True
    )


def in_order(tiles, dim):
    shape = list(tiles.shape[1:])
    shape[dim] *= tiles.shape[0]
    return jnp.moveaxis(tiles, 0, dim).reshape(shape)


def gather_axes(shard, axes, dim):
    far, near = axes
    leading = sent_to_all(shard, far)
    tiles = jnp.swapaxes(sent_to_all(leading, near), 0, 1)
    return in_order(tiles.reshape(-1, *shard.shape), dim)


def nested_sum(shard, axes):
    lines = shard.reshape(-1, shard.shape[-1])
    own = summed_rows(padded_to(lines, lax.axis_size(axes[0]) * lax.axis_size(axes[1])), axes, 0)
    whole = gather_axes(own, axes, 0)
    return whole[: len(lines)].reshape(shard.shape)


def selector(block_sizes, total, count, width):
    offsets = jnp.cumsum(block_sizes) - block_sizes
    column = jnp.arange(total, dtype=jnp.int32)[:, None, None]
    inside = jnp.arange(width, dtype=jnp.int32)[None, None, :]
    hit = (column == offsets[None, :, None] + inside) & (inside < block_sizes[None, :, None])
    return hit.astype(jnp.bfloat16).reshape(total, count * width)


def subspace(cover, block_sizes, keep_count, start_block):
    width = cover.shape[1]
    ranks = start_block.shape[2]
    inside = jnp.arange(width, dtype=jnp.int32)[None, :, None] < block_sizes[:, None, None]
    keep = jnp.minimum(keep_count, (block_sizes + 1) // 2)
    current = jnp.where(inside, start_block, jnp.zeros_like(start_block))
    for turn in range(ITERS):
        product = jnp.einsum("bij,bjk->bik", cover, current, precision=HIGH)
        columns = []
        for column_id in range(ranks):
            vector = product[:, :, column_id]
            for earlier in columns:
                vector = vector - jnp.sum(earlier * vector, axis=1, keepdims=True) * earlier
            length = jnp.sqrt(jnp.sum(vector * vector, axis=1, keepdims=True))
            alive = (column_id < keep)[:, None]
            columns.append(jnp.where(alive, vector / length, jnp.zeros_like(vector)))
        current = jnp.stack(columns, axis=2)
    product = jnp.einsum("bij,bjk->bik", cover, current, precision=HIGH)
    found = jnp.sum(current * product, axis=1)
    return (current, found)


def per_device(images, expansion_basis, block_sizes, keep_count, start_block):
    rows = images.shape[0]
    coeffs = jnp.dot(
        images,
        lax.all_gather(expansion_basis, IMG, axis=1, tiled=True),
        preferred_element_type=jnp.float32,
    ).astype(jnp.bfloat16)
    samples = coeffs.reshape(2 * rows, S)
    pick = selector(block_sizes, S, L, NMAX)
    padded = jnp.dot(samples, pick, preferred_element_type=jnp.float32).astype(jnp.bfloat16)
    wide = padded.reshape(2 * rows, L, NMAX)
    scale = 1.0 / (2 * rows * lax.axis_size(IMG) * lax.axis_size("grp"))
    partial_value = (
        jnp.einsum("rli,rlj->lij", wide, wide, preferred_element_type=jnp.float32) * scale
    )
    cover = nested_sum(partial_value, (("img_0", "img_1"), ("img_2", "grp")))
    vectors, found = subspace(cover, block_sizes, keep_count, start_block)
    rounded = vectors.astype(jnp.bfloat16)
    features = jnp.einsum("rli,lij->rlj", wide, rounded, preferred_element_type=jnp.float32)
    return (features.reshape(rows, 2 * L * KMAX), found)


def solution(mesh):
    split = Mesh(
        mesh.devices.reshape(4, 4, 2, mesh.shape["grp"]), ("img_0", "img_1", "img_2", "grp")
    )
    in_specs = (P(IMG_GRP, None), P(None, IMG), P(), P(), P())
    out_specs = (P(IMG_GRP, None), P())
    return jax.shard_map(
        per_device, mesh=split, in_specs=in_specs, out_specs=out_specs, check_vma=False
    )
```

profile of v0, /device:TPU:1, one launch (start us, length us, event | category | flops | bytes accessed | tf_op | source)
XLA Modules:
  0.0 224.9 jit_solution(15298328586002970351)
XLA Ops:
  7.2 0.7 all-gather.3.cloned.1.call-update
  7.9 0.7 copy.372
  8.8 0.7 sub.680
  9.4 0.8 broadcast_reduce_fusion
  10.5 80.9 %all-gather.3.cloned.1.call-done = bf16[32,30,9216]{2,1,0:T(8,128)(2,1)} async-done(((bf16[1,30,9216]{2,1,0:T(8,128)(2,1)}), bf16[32,30,9216]{2,1,0:T(8,128)(2,1)}) %all-gather.3.cloned.1.call-update) | async-done | bytes 17694736 | tf_op jit(solution)/shard_map/all_gather | solution.py:103
  91.4 16.4 %reshape.2849 = bf16[960,9216]{1,0:T(8,128)(2,1)} reshape(bf16[32,30,9216]{2,1,0:T(8,128)(2,1)} %all-gather.3.cloned.1.call-done) | data formatting | bytes 35389440
  107.8 15.0 %convolution_convert_fusion.1 = bf16[384,960]{0,1:T(8,128)(2,1)S(1)} fusion(bf16[384,9216]{1,0:T(8,128)(2,1)} %param.5, bf16[960,9216]{1,0:T(8,128)(2,1)} %reshape.2849), kind=kOutput, calls=%fused_computation.3 | convolution fusion | flops 6795141120 | bytes 25509888 | tf_op jit(solution)/shard_map/dot_general | solution.py:101
  122.8 0.3 copy.371
  123.1 0.5 reshape.2843
  123.6 2.5 %convolution_convert_fusion = bf16[768,1280]{1,0:T(8,128)(2,1)} fusion(bf16[768,480]{1,0:T(8,128)(2,1)S(1)} %reshape.2843, s32[1280]{0:T(1024)S(1)} %add.35, pred[1280]{0:T(1024)(128)(4,1)S(1)} %lt.38), kind=kOutput, calls=%fused_computation | convolution fusion | flops 945930240 | bytes 2709760 | tf_op jit(solution)/shard_map/dot_general | solution.py:108
  126.2 2.7 %copy.373 = bf16[768,1280]{0,1:T(8,128)(2,1)S(1)} copy(bf16[768,1280]{1,0:T(8,128)(2,1)} %convolution_convert_fusion) | data formatting | bytes 3932160 | tf_op jit(solution)/shard_map/convert_element_type | solution.py:108
  128.8 0.7 convolution_multiply_fusion
  129.7 15.1 %all_to_all.20 = f32[8,16,10,80]{3,1,2,0:T(8,128)S(1)} all-to-all(f32[8,16,10,80]{3,1,2,0:T(8,128)S(1)} %bitcast.97), channel_id=1, replica_groups=mesh['img_0'=4,'img_1'=4,'img_2'=2,'grp'=4] {'img_2','grp'}, dimensions={0} | all-to-all | bytes 819200 | tf_op jit(solution)/shard_map/all_to_all | solution.py:25
  145.1 11.1 %all_to_all.21 = f32[16,1,800]{2,1,0:T(1,128)S(1)} all-to-all(f32[16,1,800]{2,1,0:T(1,128)S(1)} %reshape.2863), channel_id=1, replica_groups=mesh['img_0'=4,'img_1'=4,'img_2'=2,'grp'=4] {'img_0','img_1'}, dimensions={0} | all-to-all | bytes 102400 | tf_op jit(solution)/shard_map/all_to_all | solution.py:33
  156.2 0.5 broadcast.2933
  156.7 0.8 reduce.9
  157.7 0.8 reshape.2865
  158.4 3.5 %all-to-all-start.2 = ((f32[16,1,800]{2,1,0:T(1,128)}), f32[16,1,800]{2,1,0:T(1,128)S(1)}, u32[]{:S(2)}, u32[]{:S(2)}) async-start(f32[16,1,800]{2,1,0:T(1,128)} %reshape.2865), calls=%async_computation.2 | async-start | bytes 114688 | tf_op jit(solution)/shard_map/all_to_all | solution.py:44
  162.0 6.4 %all-to-all-done.2 = f32[16,1,800]{2,1,0:T(1,128)S(1)} async-done(((f32[16,1,800]{2,1,0:T(1,128)}), f32[16,1,800]{2,1,0:T(1,128)S(1)}, u32[]{:S(2)}, u32[]{:S(2)}) %all-to-all-start.2) | async-done | bytes 51232 | tf_op jit(solution)/shard_map/all_to_all | solution.py:44
  168.4 0.8 reduce.10
  169.3 0.9 broadcast_in_dim.121
  170.2 6.4 %all-to-all-start.3 = ((f32[8,16,10,80]{3,1,2,0:T(8,128)}), f32[8,16,10,80]{3,1,2,0:T(8,128)S(1)}, u32[]{:S(2)}, u32[]{:S(2)}) async-start(f32[8,16,10,80]{3,1,2,0:T(8,128)} %broadcast_in_dim.121), calls=%async_computation.3 | async-start | bytes 1310720 | tf_op jit(solution)/shard_map/all_to_all | solution.py:44
  176.7 10.7 %all-to-all-done.3 = f32[8,16,10,80]{3,1,2,0:T(8,128)S(1)} async-done(((f32[8,16,10,80]{3,1,2,0:T(8,128)}), f32[8,16,10,80]{3,1,2,0:T(8,128)S(1)}, u32[]{:S(2)}, u32[]{:S(2)}) %all-to-all-start.3) | async-done | bytes 409632 | tf_op jit(solution)/shard_map/all_to_all | solution.py:44
  187.4 1.3 fusion.6
  189.1 0.2 multiply_reduce_fusion.79
  189.4 0.3 multiply_reduce_fusion.78
  190.1 0.3 multiply_reduce_fusion.77
  190.4 0.2 multiply_reduce_fusion.76
  191.0 0.2 multiply_reduce_fusion.75
  192.9 0.2 constant_dynamic-update-slice_fusion
  193.1 1.3 fusion.8
  194.9 0.2 multiply_reduce_fusion.43
  195.1 0.3 multiply_reduce_fusion.42
  195.8 0.3 multiply_reduce_fusion.41
  196.1 0.2 multiply_reduce_fusion.40
  196.7 0.2 multiply_reduce_fusion.39
  198.6 0.2 constant_dynamic-update-slice_fusion.8
  198.8 1.3 fusion.10
  200.6 0.2 multiply_reduce_fusion.7
  200.8 0.3 multiply_reduce_fusion.6
  201.5 0.3 multiply_reduce_fusion.5
  202.5 0.2 multiply_reduce_fusion.3
  204.3 0.2 constant_dynamic-update-slice_fusion.16
  204.6 1.3 fusion.4
  205.9 0.7 fusion.12
  206.6 0.4 convolution_bitcast_fusion
  206.9 4.9 %copy.407 = f32[768,16,8]{2,1,0:T(8,128)} copy(f32[768,16,8]{0,2,1:T(8,128)S(1)} %convolution_bitcast_fusion) | data formatting | bytes 786432 | tf_op jit(solution)/shard_map/rli,lij->rlj/transpose | solution.py:117
  211.8 6.3 %reshape.2847 = f32[384,256]{1,0:T(8,128)} reshape(f32[768,16,8]{2,1,0:T(8,128)} %copy.407) | data formatting | bytes 786432 | tf_op jit(solution)/shard_map/reshape | solution.py:118
  (106 shorter events, 10.0 us)
Async XLA Ops:
  7.2 84.2 %all-gather.3.cloned.1.call-start = ((), (), s32[]{:S(2)}) async-start(), calls=%async_computation.4 | async-start | bytes 19464192 | tf_op jit(solution)/shard_map/all_gather | solution.py:103
  129.5 32.4 %copy-start.1 = (s32[16]{0:T(128)S(1)}, s32[16]{0:T(128)}, u32[]{:S(2)}) copy-start(s32[16]{0:T(128)} %param.7) | copy-start | bytes 196
  144.8 31.8 %copy-start.2 = (s32[16]{0:T(128)S(1)}, s32[16]{0:T(128)}, u32[]{:S(2)}) copy-start(s32[16]{0:T(128)} %param.8) | copy-start | bytes 196
  144.8 42.6 %copy-start = (f32[16,80,8]{1,2,0:T(8,128)S(1)}, f32[16,80,8]{1,2,0:T(8,128)}, u32[]{:S(2)}) copy-start(f32[16,80,8]{1,2,0:T(8,128)} %param.9) | copy-start | bytes 122884
  158.4 10.0 %all-to-all-start.2 = ((f32[16,1,800]{2,1,0:T(1,128)}), f32[16,1,800]{2,1,0:T(1,128)S(1)}, u32[]{:S(2)}, u32[]{:S(2)}) async-start(f32[16,1,800]{2,1,0:T(1,128)} %reshape.2865), calls=%async_computation.2 | async-start | bytes 114688 | tf_op jit(solution)/shard_map/all_to_all | solution.py:44
  170.2 17.2 %all-to-all-start.3 = ((f32[8,16,10,80]{3,1,2,0:T(8,128)}), f32[8,16,10,80]{3,1,2,0:T(8,128)S(1)}, u32[]{:S(2)}, u32[]{:S(2)}) async-start(f32[8,16,10,80]{3,1,2,0:T(8,128)} %broadcast_in_dim.121), calls=%async_computation.3 | async-start | bytes 1310720 | tf_op jit(solution)/shard_map/all_to_all | solution.py:44
Sparse Core Ops, SparseCore 0:
  10.2 81.1 all-gather.2
where the time goes:
time: 226 us; the launch traced here: 225 us
  waiting for transfers between devices  98.7 us (44%)
  local copies, waits for them, and re-layouts  35.9 us (16%)
  blocking collectives  26.2 us (12%)
  matrix products  23.7 us (10%)
  other arithmetic  15.9 us (7%)
  between operations  14.5 us (6%)
  starting transfers between devices  9.98 us (4%)
    all_gather x1, waiting for transfers between devices, per_device(): lax.all_gather(expansion_basis, IMG, axis=1, tiled=True)  80.9 us
    unnamed x11, local copies, waits for them, and re-layouts  17.5 us
    all_to_all x2, waiting for transfers between devices, sent_to_all(): lax.all_to_all(jnp.broadcast_to(shard[None], (peers, *shard.shape)), axis...  17.1 us
    all_to_all x1, blocking collectives, sum_at_owner(): tiles = lax.all_to_all(cut_along(shard, dim, peers), axis, 0, 0, tiled=True)  15.1 us
    dot_general x1, matrix products, per_device(): jnp.dot(images, lax.all_gather(expansion_basis, IMG, axis=1, tiled=True),...  15 us
    all_to_all x1, blocking collectives, summed_rows(): lax.all_to_all(nearer, far, split_axis=0, concat_axis=0, tiled=True)  11.1 us
    all_to_all x2, starting transfers between devices, sent_to_all(): lax.all_to_all(jnp.broadcast_to(shard[None], (peers, *shard.shape)), axis...  9.94 us
    reduce_sum x30, other arithmetic, subspace(): vector = vector - jnp.sum(earlier * vector, axis=1, keepdims=True) * earlier  6.8 us
  transfers between devices with their start and end apart: 3, of which 3 were waited for; matrix products, arithmetic and copies ran while one was open for 1% of the time, Pallas kernels for 0%

commit v1 on v0

--- a/solution.py
+++ b/solution.py
@@ -100,7 +100,9 @@
     rows = images.shape[0]
     coeffs = jnp.dot(
         images,
-        lax.all_gather(expansion_basis, IMG, axis=1, tiled=True),
+        jnp.concatenate(
+            lax.all_to_all(jnp.stack([expansion_basis] * lax.axis_size(IMG)), IMG, 0, 0), axis=1
+        ),
         preferred_element_type=jnp.float32,
     ).astype(jnp.bfloat16)
     samples = coeffs.reshape(2 * rows, S)

time: 226 us -> 449 us (1.99)
  waiting for transfers between devices: 98.7 us -> 279 us
  blocking collectives: 26.2 us -> 67.4 us
  between operations: 14.5 us -> 1.1 us
  starting transfers between devices: 9.98 us -> 19.7 us
  local copies, waits for them, and re-layouts: 35.9 us -> 42.3 us
    all_to_all x0 -> x1, waiting for transfers between devices: none -> 262 us  [per_device(): lax.all_to_all(jnp.stack([expansion_basis] * lax.axis_size(IMG)), IMG, 0, 0)]
    all_gather x1 -> x0, waiting for transfers between devices: 80.9 us -> none  [per_device(): lax.all_gather(expansion_basis, IMG, axis=1, tiled=True)]
    all_to_all x1, blocking collectives: 11.1 us -> 44.7 us  [summed_rows(): lax.all_to_all(nearer, far, split_axis=0, concat_axis=0, tiled=True)]
    unnamed x11 -> x10, local copies, waits for them, and re-layouts: 17.5 us -> 1.11 us
    reshape x0 -> x1, local copies, waits for them, and re-layouts: none -> 16.4 us  [per_device(): jnp.concatenate(lax.all_to_all(jnp.stack([expansion_basis] * lax.axis_siz...]
    all_to_all x0 -> x1, starting transfers between devices: none -> 9.77 us  [per_device(): lax.all_to_all(jnp.stack([expansion_basis] * lax.axis_size(IMG)), IMG, 0, 0)]
    all_to_all x1, blocking collectives: 15.1 us -> 22.7 us  [sum_at_owner(): tiles = lax.all_to_all(cut_along(shard, dim, peers), axis, 0, 0, tiled=True)]
    another operation x1 -> x2, local copies, waits for them, and re-layouts: 0.73 us -> 7.78 us  [the longest x1 7.69 us: per_device(): jnp.stack([expansion_basis] * lax.axis_size(IMG))]
  transfers between devices with their start and end apart: 3 -> 3, of which waited for: 3 -> 3; matrix products, arithmetic and copies ran while one was open for 1% -> 0% of each run, Pallas kernels for 0% -> 0%
where the time goes in v1:
time: 449 us
  waiting for transfers between devices  279 us (62%)
  blocking collectives  67.4 us (15%)
  local copies, waits for them, and re-layouts  42.3 us (9%)
  matrix products  23.7 us (5%)
  starting transfers between devices  19.7 us (4%)
  other arithmetic  15.3 us (3%)
    all_to_all x1, waiting for transfers between devices, per_device(): lax.all_to_all(jnp.stack([expansion_basis] * lax.axis_size(IMG)), IMG, 0, 0)  262 us
    all_to_all x1, blocking collectives, summed_rows(): lax.all_to_all(nearer, far, split_axis=0, concat_axis=0, tiled=True)  44.7 us
    all_to_all x1, blocking collectives, sum_at_owner(): tiles = lax.all_to_all(cut_along(shard, dim, peers), axis, 0, 0, tiled=True)  22.7 us
    all_to_all x2, waiting for transfers between devices, sent_to_all(): lax.all_to_all(jnp.broadcast_to(shard[None], (peers, *shard.shape)), axis...  17.1 us
    reshape x1, local copies, waits for them, and re-layouts, per_device(): jnp.concatenate(lax.all_to_all(jnp.stack([expansion_basis] * lax.axis_siz...  16.4 us
    dot_general x1, matrix products, per_device(): jnp.dot(images, jnp.concatenate(lax.all_to_all(jnp.stack([expansion_basis...  15 us
    all_to_all x2, starting transfers between devices, sent_to_all(): lax.all_to_all(jnp.broadcast_to(shard[None], (peers, *shard.shape)), axis...  9.94 us
    all_to_all x1, starting transfers between devices, per_device(): lax.all_to_all(jnp.stack([expansion_basis] * lax.axis_size(IMG)), IMG, 0, 0)  9.77 us
  transfers between devices with their start and end apart: 3, of which 3 were waited for; matrix products, arithmetic and copies ran while one was open for 0% of the time, Pallas kernels for 0%

profile of v1, /device:TPU:1, one launch (start us, length us, event | category | flops | bytes accessed | tf_op | source)
XLA Modules:
  0.0 448.6 jit_solution(16894954700983877504)
XLA Ops:
  0.6 7.7 %stack.8 = bf16[32,9216,30]{1,2,0:T(8,128)(2,1)} broadcast(bf16[9216,30]{0,1:T(8,128)(2,1)} %param.6), dimensions={1,2} | broadcast | bytes 18247680 | tf_op jit(solution)/shard_map/stack | solution.py:104
  8.3 9.8 %all-to-all-start = ((bf16[32,9216,30]{1,2,0:T(8,128)(2,1)}), bf16[32,9216,30]{1,2,0:T(8,128)(2,1)}, u32[]{:S(2)}, u32[]{:S(2)}) async-start(bf16[32,9216,30]{1,2,0:T(8,128)(2,1)} %stack.8), calls=%async_computation | async-start | bytes 37748736 | tf_op jit(solution)/shard_map/all_to_all | solution.py:104
  18.7 262.0 %all-to-all-done = bf16[32,9216,30]{1,2,0:T(8,128)(2,1)} async-done(((bf16[32,9216,30]{1,2,0:T(8,128)(2,1)}), bf16[32,9216,30]{1,2,0:T(8,128)(2,1)}, u32[]{:S(2)}, u32[]{:S(2)}) %all-to-all-start) | async-done | bytes 17694752 | tf_op jit(solution)/shard_map/all_to_all | solution.py:104
  280.7 16.4 %reshape.2852 = bf16[9216,960]{0,1:T(8,128)(2,1)} reshape(bf16[9216,32,30]{0,2,1:T(8,128)(2,1)} %bitcast) | data formatting | bytes 35389440 | tf_op jit(solution)/shard_map/reshape | solution.py:103
  297.1 15.0 %convolution_convert_fusion.1 = bf16[384,960]{0,1:T(8,128)(2,1)S(1)} fusion(bf16[384,9216]{1,0:T(8,128)(2,1)} %param.5, bf16[9216,960]{0,1:T(8,128)(2,1)} %reshape.2852), kind=kOutput, calls=%fused_computation.3 | convolution fusion | flops 6795141120 | bytes 25509888 | tf_op jit(solution)/shard_map/dot_general | solution.py:101
  312.2 0.3 copy.372
  312.5 0.5 reshape.2853
  312.9 2.5 convolution_convert_fusion
  315.5 2.7 copy.374
  318.2 0.7 convolution_multiply_fusion
  318.8 0.2 copy.375
  319.1 22.7 %all_to_all.25 = f32[8,16,10,80]{3,1,2,0:T(8,128)S(1)} all-to-all(f32[8,16,10,80]{3,1,2,0:T(8,128)S(1)} %bitcast.97), channel_id=1, replica_groups=mesh['img_0'=4,'img_1'=4,'img_2'=2,'grp'=4] {'img_2','grp'}, dimensions={0} | all-to-all | bytes 819200 | tf_op jit(solution)/shard_map/all_to_all | solution.py:25
  342.0 44.7 %all_to_all.26 = f32[16,1,800]{2,1,0:T(1,128)S(1)} all-to-all(f32[16,1,800]{2,1,0:T(1,128)S(1)} %reshape.2871), channel_id=1, replica_groups=mesh['img_0'=4,'img_1'=4,'img_2'=2,'grp'=4] {'img_0','img_1'}, dimensions={0} | all-to-all | bytes 102400 | tf_op jit(solution)/shard_map/all_to_all | solution.py:33
  386.7 0.5 broadcast.2935
  387.2 0.8 reduce.9
  388.2 0.8 reshape.2873
  388.9 3.5 all-to-all-start.3
  392.5 6.4 %all-to-all-done.3 = f32[16,1,800]{2,1,0:T(1,128)S(1)} async-done(((f32[16,1,800]{2,1,0:T(1,128)}), f32[16,1,800]{2,1,0:T(1,128)S(1)}, u32[]{:S(2)}, u32[]{:S(2)}) %all-to-all-start.3) | async-done | bytes 51232 | tf_op jit(solution)/shard_map/all_to_all | solution.py:44
  398.9 0.8 reduce.10
  399.8 0.9 broadcast_in_dim.121
  400.7 6.4 %all-to-all-start.4 = ((f32[8,16,10,80]{3,1,2,0:T(8,128)}), f32[8,16,10,80]{3,1,2,0:T(8,128)S(1)}, u32[]{:S(2)}, u32[]{:S(2)}) async-start(f32[8,16,10,80]{3,1,2,0:T(8,128)} %broadcast_in_dim.121), calls=%async_computation.4 | async-start | bytes 1310720 | tf_op jit(solution)/shard_map/all_to_all | solution.py:44
  407.2 10.7 %all-to-all-done.4 = f32[8,16,10,80]{3,1,2,0:T(8,128)S(1)} async-done(((f32[8,16,10,80]{3,1,2,0:T(8,128)}), f32[8,16,10,80]{3,1,2,0:T(8,128)S(1)}, u32[]{:S(2)}, u32[]{:S(2)}) %all-to-all-start.4) | async-done | bytes 409632 | tf_op jit(solution)/shard_map/all_to_all | solution.py:44
  417.9 1.3 fusion.6
  419.6 0.2 multiply_reduce_fusion.79
  419.9 0.3 multiply_reduce_fusion.78
  420.6 0.3 multiply_reduce_fusion.77
  420.9 0.2 multiply_reduce_fusion.76
  421.5 0.2 multiply_reduce_fusion.75
  423.4 0.2 constant_dynamic-update-slice_fusion
  423.6 1.3 fusion.8
  425.4 0.2 multiply_reduce_fusion.43
  425.6 0.3 multiply_reduce_fusion.42
  426.3 0.3 multiply_reduce_fusion.41
  426.6 0.2 multiply_reduce_fusion.40
  427.2 0.2 multiply_reduce_fusion.39
  429.1 0.2 constant_dynamic-update-slice_fusion.8
  429.3 1.3 fusion.10
  431.1 0.2 multiply_reduce_fusion.7
  431.3 0.3 multiply_reduce_fusion.6
  432.0 0.3 multiply_reduce_fusion.5
  432.3 0.2 multiply_reduce_fusion.4
  433.0 0.2 multiply_reduce_fusion.3
  434.8 0.2 constant_dynamic-update-slice_fusion.16
  435.1 1.3 fusion.4
  436.4 0.7 fusion.12
  437.1 0.4 convolution_bitcast_fusion
  437.4 4.9 %copy.408 = f32[768,16,8]{2,1,0:T(8,128)} copy(f32[768,16,8]{0,2,1:T(8,128)S(1)} %convolution_bitcast_fusion) | data formatting | bytes 786432 | tf_op jit(solution)/shard_map/rli,lij->rlj/transpose | solution.py:119
  442.3 6.3 %reshape.2857 = f32[384,256]{1,0:T(8,128)} reshape(f32[768,16,8]{2,1,0:T(8,128)} %copy.408) | data formatting | bytes 786432 | tf_op jit(solution)/shard_map/reshape | solution.py:120
  (106 shorter events, 9.7 us)
Async XLA Ops:
  8.3 9.8 %copy-start.1 = (s32[16]{0:T(128)S(1)}, s32[16]{0:T(128)}, u32[]{:S(2)}) copy-start(s32[16]{0:T(128)} %param.7) | copy-start | bytes 196
  8.3 272.4 %all-to-all-start = ((bf16[32,9216,30]{1,2,0:T(8,128)(2,1)}), bf16[32,9216,30]{1,2,0:T(8,128)(2,1)}, u32[]{:S(2)}, u32[]{:S(2)}) async-start(bf16[32,9216,30]{1,2,0:T(8,128)(2,1)} %stack.8), calls=%async_computation | async-start | bytes 37748736 | tf_op jit(solution)/shard_map/all_to_all | solution.py:104
  341.8 65.3 %copy-start.2 = (s32[16]{0:T(128)S(1)}, s32[16]{0:T(128)}, u32[]{:S(2)}) copy-start(s32[16]{0:T(128)} %param.8) | copy-start | bytes 196
  341.8 76.1 %copy-start = (f32[16,80,8]{1,2,0:T(8,128)S(1)}, f32[16,80,8]{1,2,0:T(8,128)}, u32[]{:S(2)}) copy-start(f32[16,80,8]{1,2,0:T(8,128)} %param.9) | copy-start | bytes 122884
  388.9 10.0 %all-to-all-start.3 = ((f32[16,1,800]{2,1,0:T(1,128)}), f32[16,1,800]{2,1,0:T(1,128)S(1)}, u32[]{:S(2)}, u32[]{:S(2)}) async-start(f32[16,1,800]{2,1,0:T(1,128)} %reshape.2873), calls=%async_computation.3 | async-start | bytes 114688 | tf_op jit(solution)/shard_map/all_to_all | solution.py:44
  400.7 17.2 %all-to-all-start.4 = ((f32[8,16,10,80]{3,1,2,0:T(8,128)}), f32[8,16,10,80]{3,1,2,0:T(8,128)S(1)}, u32[]{:S(2)}, u32[]{:S(2)}) async-start(f32[8,16,10,80]{3,1,2,0:T(8,128)} %broadcast_in_dim.121), calls=%async_computation.4 | async-start | bytes 1310720 | tf_op jit(solution)/shard_map/all_to_all | solution.py:44
